TPU v7x, 32 devices: a whole 2x2x4 slice. The times are simulated.
32 devices in a mesh: gy: 4 (over z), gx: 8 (over y, x, core).
Axes of the slice: x: 2, y: 2, z: 4, core: 2. Of those that a mesh axis runs over, the one named last changes fastest.
Arguments:
- height: float32 [384, 512], P('gx', 'gy'), may hold values from -6 to 6
- east_speed: float32 [384, 512], P('gx', 'gy'), may hold values from -3 to 3
- north_speed: float32 [384, 512], P('gx', 'gy'), may hold values from -3 to 3
- water_depth: float32 [384, 512], P('gx', 'gy'), may hold values from 0.5 to 2
- ocean_mask: int32 [384, 512], P('gx', 'gy'), may hold values 0 or 1
- fold_partner: int32 [8], replicated, may hold values from 0 to 7, each once
- love_factor: float32 [360], replicated, may hold values from 0.1 to 1
Outputs:
- sal_field: float32 [384, 512], P('gx', 'gy')
- east_next: float32 [384, 512], P('gx', 'gy')
- north_next: float32 [384, 512], P('gx', 'gy')
- height_next: float32 [384, 512], P('gx', 'gy')
Inputs may be any that keep to these rules, and one draw needn't show every extreme that they name: `fold_partner`: a permutation of the tile columns.
All inputs are finite; a program needn't handle non-finite values. No bound on the sum of `ocean_mask` on one device may be relied on, other than what follows from the above.
Results may differ from a plain program's by a relative error of at most 0.00055.
Values sent between devices are 32-bit elements; how exact they have to be, the bound alone decides.
A program may use at most 64 MiB of HBM per device.

v0:
```python
import math

import jax
import jax.numpy as jnp
from jax import lax
from jax.sharding import PartitionSpec as P

COURANT = 0.35


def with_halo(shard, sides, width):
    for axis, dim in sides:
        size, length = (lax.axis_size(axis), shard.shape[dim])
        up = [(i, (i + 1) % size) for i in range(size)]
        down = [(j, i) for i, j in up]
        last = lax.slice_in_dim(shard, length - width, length, axis=dim)
        first = lax.slice_in_dim(shard, 0, width, axis=dim)
        before = lax.ppermute(last, axis, up)
        after = lax.ppermute(first, axis, down)
        shard = jnp.concatenate([before, shard, after], axis=dim)
    return shard


def latitude_rows(number, lat_total, lon_total):
    rows_float = jnp.arange(number, dtype=jnp.int32).astype(jnp.float32)
    colatitude = math.pi * (rows_float + 0.5) / lat_total
    sines = jnp.sin(colatitude)
    quadrature = math.pi / lat_total * (2.0 * math.pi / lon_total) * sines
    return (jnp.cos(colatitude), sines, quadrature)


def seed_for_orders(sines, order_ints, slot_count):
    factors = jnp.arange(1, slot_count, dtype=jnp.float32)
    increments = 0.5 * jnp.log((2.0 * factors + 1.0) / (2.0 * factors))
    seed_logs = jnp.concatenate([jnp.zeros((1,), jnp.float32), jnp.cumsum(increments)])
    table_index = jnp.arange(slot_count, dtype=jnp.int32)
    picked = jnp.sum(
        jnp.where(table_index[:, None] == order_ints[None, :], seed_logs[:, None], 0.0), axis=0
    )
    exponent = order_ints.astype(jnp.float32)[None, :] * jnp.log(sines)[:, None] + picked[None, :]
    log_shift = jnp.clip(-exponent - 80.0, 0.0, 80.0)
    return (jnp.exp(exponent + log_shift) * (1.0 / math.sqrt(4.0 * math.pi)), jnp.exp(-log_shift))


def order_of_slots(first_slot, count, per_device, devices_all):
    slots = first_slot + jnp.arange(count, dtype=jnp.int32)
    owner = slots // per_device
    within = slots % per_device
    return within * devices_all + jnp.where(within % 2 == 0, owner, devices_all - 1 - owner)


def legendre_next(carry, degree, cosines, seed_rows, orders):
    previous, before = carry
    degree_value = degree.astype(jnp.float32)
    below_value = degree_value - 1.0
    growth = jnp.sqrt(
        jnp.maximum(4.0 * degree_value * degree_value - 1.0, 1.0)
        / jnp.maximum(degree_value * degree_value - orders * orders, 1.0)
    )
    damping = jnp.sqrt(
        jnp.maximum(below_value * below_value - orders * orders, 0.0)
        / jnp.maximum(4.0 * below_value * below_value - 1.0, 1.0)
    )
    stepped = growth[None, :] * (cosines[:, None] * previous - damping[None, :] * before)
    values = jnp.where(
        degree_value == orders[None, :],
        seed_rows,
        jnp.where(degree_value > orders[None, :], stepped, 0.0),
    )
    return ((values, previous), values)


def partner_rows(all_rows, fold_partner, lon_index, tile_lon):
    offset = fold_partner[lon_index] * tile_lon
    chosen = lax.dynamic_slice_in_dim(all_rows, offset, tile_lon, 1)
    return chosen[:, ::-1]


def with_north(extended, fold_values, is_top):
    channels = fold_values.shape[0]
    north_rim = extended[:channels, 1:-1, -1]
    return extended.at[:channels, 1:-1, -1].set(jnp.where(is_top, fold_values, north_rim))


def on_device(height, east_speed, north_speed, water_depth, ocean_mask, fold_partner, love_factor):
    tile_lon, tile_lat = height.shape
    degrees = love_factor.shape[0]
    lon_devices = lax.axis_size("gx")
    lat_devices = lax.axis_size("gy")
    lon_index = lax.axis_index("gx")
    lat_index = lax.axis_index("gy")
    lon_count = tile_lon * lon_devices
    lat_count = tile_lat * lat_devices
    is_top = lat_index == lat_devices - 1
    wet_cells = ocean_mask.astype(jnp.float32)
    surface = wet_cells * height
    devices_all = lon_devices * lat_devices
    per_device = (degrees + devices_all - 1) // devices_all
    slot_count = per_device * devices_all
    tile_columns = lon_index * tile_lon + jnp.arange(tile_lon, dtype=jnp.int32)

    def order_trig(first_slot, count):
        slot_orders = order_of_slots(first_slot, count, per_device, devices_all)
        phases = tile_columns[:, None] * slot_orders[None, :] % lon_count
        angles = phases.astype(jnp.float32) * (2.0 * math.pi / lon_count)
        return (jnp.cos(angles), jnp.sin(angles))

    cos_cols, sin_cols = order_trig(jnp.int32(0), slot_count // lon_devices * lax.axis_size("gx"))
    cos_rows = lax.dot_general(
        cos_cols,
        surface,
        (((0,), (0,)), ((), ())),
        precision=lax.Precision.HIGHEST,
        preferred_element_type=jnp.float32,
    )
    sin_rows = lax.dot_general(
        sin_cols,
        surface,
        (((0,), (0,)), ((), ())),
        precision=lax.Precision.HIGHEST,
        preferred_element_type=jnp.float32,
    )
    order_sums = lax.psum_scatter(
        jnp.stack([cos_rows, sin_rows], axis=1), "gx", scatter_dimension=0, tiled=True
    )
    by_order = lax.all_to_all(order_sums, "gy", split_axis=0, concat_axis=2, tiled=True)
    my_first = (lon_index * lat_devices + lat_index) * per_device
    my_order_ints = order_of_slots(my_first, per_device, per_device, devices_all)
    my_orders = my_order_ints.astype(jnp.float32)
    all_cosines, all_sines, all_weights = latitude_rows(lat_count, lat_count, lon_count)
    order_seeds, order_unscale = seed_for_orders(all_sines, my_order_ints, slot_count)
    order_empty = jnp.zeros((lat_count, per_device), jnp.float32)

    def order_advance(carry, degree):
        return legendre_next(carry, degree, all_cosines, order_seeds, my_orders)

    order_done, order_scaled_legendre = lax.scan(
        order_advance, (order_empty, order_empty), jnp.arange(degrees, dtype=jnp.int32)
    )
    order_legendre = order_scaled_legendre * order_unscale[None]
    order_weighted = by_order * all_weights[None, None, :]
    order_spectrum = jnp.einsum(
        "ljs,scj->cls", order_legendre, order_weighted, precision=lax.Precision.HIGHEST
    )
    order_mult = jnp.where(my_order_ints == 0, 1.0, 2.0).astype(jnp.float32)
    order_scaled = order_spectrum * love_factor[None, :, None] * order_mult[None, None, :]
    order_grid = jnp.einsum(
        "cls,ljs->scj", order_scaled, order_legendre, precision=lax.Precision.HIGHEST
    )
    returned = lax.all_to_all(order_grid, "gy", split_axis=2, concat_axis=0, tiled=True)
    piece = lax.all_gather(returned, "gx", axis=0, tiled=True)
    cos_cols, sin_cols = order_trig(jnp.int32(0), piece.shape[0])
    cos_add = jnp.dot(
        cos_cols,
        piece[:, 0, :],
        precision=lax.Precision.HIGHEST,
        preferred_element_type=jnp.float32,
    )
    sin_add = jnp.dot(
        sin_cols,
        piece[:, 1, :],
        precision=lax.Precision.HIGHEST,
        preferred_element_type=jnp.float32,
    )
    sal_field = cos_add + sin_add
    mixed = jnp.stack([surface - sal_field, water_depth, wet_cells, east_speed, north_speed])
    mixed_ext = with_halo(mixed, (("gy", 2), ("gx", 1)), 1)
    mixed_top = lax.all_gather(mixed[:3, :, -1], "gx", axis=1, tiled=True)
    mixed_ext = with_north(
        mixed_ext, partner_rows(mixed_top, fold_partner, lon_index, tile_lon), is_top
    )
    pressure_ext = mixed_ext[0]
    depth_ext = mixed_ext[1]
    wet_ext = mixed_ext[2]
    east_ext = mixed_ext[3]
    north_ext = mixed_ext[4]
    east_faces = (
        wet_ext[:-1, 1:-1]
        * wet_ext[1:, 1:-1]
        * (east_ext[:-1, 1:-1] - COURANT * (pressure_ext[1:, 1:-1] - pressure_ext[:-1, 1:-1]))
    )
    north_faces = (
        wet_ext[1:-1, :-1]
        * wet_ext[1:-1, 1:]
        * (north_ext[1:-1, :-1] - COURANT * (pressure_ext[1:-1, 1:] - pressure_ext[1:-1, :-1]))
    )
    east_flux = 0.5 * (depth_ext[:-1, 1:-1] + depth_ext[1:, 1:-1]) * east_faces
    north_flux = 0.5 * (depth_ext[1:-1, :-1] + depth_ext[1:-1, 1:]) * north_faces
    bottom_gate = jnp.where(lat_index > 0, 1.0, 0.0).astype(jnp.float32)
    south_flux = jnp.concatenate([north_flux[:, :1] * bottom_gate, north_flux[:, 1:-1]], axis=1)
    height_next = wet_cells * (
        surface - COURANT * (east_flux[1:] - east_flux[:-1] + north_flux[:, 1:] - south_flux)
    )
    return (sal_field, east_faces[1:], north_faces[:, 1:], height_next)


def solution(mesh):
    in_specs = (P("gx", "gy"), P("gx", "gy"), P("gx", "gy"), P("gx", "gy"), P("gx", "gy"), P(), P())
    out_specs = (P("gx", "gy"), P("gx", "gy"), P("gx", "gy"), P("gx", "gy"))
    return jax.shard_map(
        on_device, mesh=mesh, in_specs=in_specs, out_specs=out_specs, check_vma=False
    )
```

profile of v0, /device:TPU:0, one launch (start us, length us, event | category | flops | bytes accessed | tf_op | source)
XLA Modules:
  0.0 867.2 jit_solution(15962236669647059883)
XLA Ops:
  7.2 1.6 convolution_bitcast_fusion
  8.8 1.6 convolution_bitcast_fusion.1
  10.4 0.8 pad_maximum_fusion
  12.4 743.4 %while.21 = (s32[]{:T(128)}, f32[512,12]{0,1:T(8,128)S(1)}, f32[512,12]{0,1:T(8,128)S(1)}, f32[360,512,12]{1,2,0:T(8,128)}, s32[360]{0:T(512)S(1)}, /*index=5*/s...) while((s32[]{:T(128)}, f32[512,12]{0,1:T(8,128)S(1)}, ...), condition=%wide.region_5.6_spmd.clone.clone.clone, body=%wide.region_4.5_spmd.clone.clone.clone.sunk | while | flops 88395 | bytes 138387 | solution.py:137
  585.7 0.7 bitcast_dynamic-update-slice_fusion.4
  755.7 11.7 %broadcast_multiply_fusion = f32[360,512,12]{1,2,0:T(8,128)} fusion(f32[360,512,12]{1,2,0:T(8,128)} %get-tuple-element.151, f32[512,12]{0,1:T(8,128)S(1)} %negate_exponential_fusion), kind=kLoop, calls=%fused_computation.33 | loop fusion | flops 2211840 | bytes 17719296 | tf_op jit(solution)/shard_map/mul | solution.py:140
  767.5 1.5 copy.39
  768.9 6.4 all-to-all-start
  775.3 5.7 all-to-all-done
  781.0 15.9 %fusion.22 = f32[2,360,12]{1,0,2:T(2,128)S(1)} fusion(f32[360,512,12]{1,2,0:T(8,128)} %broadcast_multiply_fusion, f32[4,12,1,2,128]{4,3,2,1,0:T(2,128)S(1)} %bitcast.72, f32[512]{0:T(512)S(1)} %fusion.84, f32[12]{0:T(128)S(1)} %compare_select_fusion.8, f32[360]{0:T(512)S(1)} %copy-done.6), kind=kOutput, calls=%fused_computation.38 | convolution fusion | flops 53113728 | bytes 8934608 | tf_op jit(solution)/shard_map/ljs,scj->cls/dot_general | solution.py:142
  796.9 13.4 %fusion.12 = f32[12,2,512]{2,1,0:T(2,128)S(1)} fusion(f32[2,360,12]{1,0,2:T(2,128)S(1)} %fusion.22, f32[360,512,12]{1,2,0:T(8,128)} %broadcast_multiply_fusion), kind=kOutput, calls=%fused_computation.29 | convolution fusion | flops 53084160 | bytes 8931072 | tf_op jit(solution)/shard_map/cls,ljs->scj/dot_general | solution.py:147
  810.6 1.4 reshape.356
  812.1 3.3 all-to-all-start.1
  816.6 4.4 all-to-all-done.1
  821.5 0.8 reduce.8
  822.3 0.8 reshape.357
  823.3 9.6 %all_gather.6 = f32[384,2,128]{2,1,0:T(2,128)S(1)} all-gather(f32[48,2,128]{2,1,0:T(2,128)S(1)} %bitcast.73), channel_id=1, replica_groups=mesh['gy'=4,'gx'=8] {'gx'}, dimensions={0}, use_global_device_ids=true | all-gather | bytes 442368 | tf_op jit(solution)/shard_map/all_gather | solution.py:151
  834.6 0.7 collective-permute-start.1
  835.5 10.0 %all-gather = f32[3,384,1]{2,1,0:T(8,128)S(1)} all-gather(f32[3,48,1]{2,1,0:T(8,128)S(1)} %pad_maximum_fusion.2), channel_id=2, replica_groups=mesh['gy'=4,'gx'=8] {'gx'}, dimensions={1}, use_global_device_ids=true | all-gather | bytes 5184 | tf_op jit(solution)/shard_map/all_gather | solution.py:168
  845.4 1.3 collective-permute-start
  847.0 5.8 collective-permute-done
  853.0 2.6 collective-permute-start.3
  855.8 1.1 collective-permute-done.2
  857.1 0.9 scatter.4
  (1871 shorter events, 507.8 us)
Async XLA Ops:
  7.2 760.3 %reduce-scatter.2.cloned.1.call-start = ((), (), s32[]{:S(2)}) async-start(), calls=%async_computation.3 | async-start | bytes 442368 | tf_op jit(solution)/shard_map/reduce_scatter | solution.py:123
  755.7 25.3 %copy-start.6 = (f32[360]{0:T(512)S(1)}, f32[360]{0:T(512)}, u32[]{:S(2)}) copy-start(f32[360]{0:T(512)} %param.17) | copy-start | bytes 4324
  767.4 47.9 %copy-start = (s32[48,128]{1,0:T(8,128)S(1)}, s32[48,128]{1,0:T(8,128)}, u32[]{:S(2)}) copy-start(s32[48,128]{1,0:T(8,128)} %param.15) | copy-start | bytes 73732
  767.4 47.9 %copy-start.7 = (s32[8]{0:T(128)S(1)}, s32[8]{0:T(128)}, u32[]{:S(2)}) copy-start(s32[8]{0:T(128)} %param.16) | copy-start | bytes 100
  767.4 67.0 %copy-start.1 = (f32[48,128]{1,0:T(8,128)S(1)}, f32[48,128]{1,0:T(8,128)}, u32[]{:S(2)}) copy-start(f32[48,128]{1,0:T(8,128)} %param.11) | copy-start | bytes 73732
  767.4 67.0 %copy-start.2 = (f32[48,128]{1,0:T(8,128)S(1)}, f32[48,128]{1,0:T(8,128)}, u32[]{:S(2)}) copy-start(f32[48,128]{1,0:T(8,128)} %param.14) | copy-start | bytes 73732
  767.4 67.1 %copy-start.4 = (f32[48,128]{1,0:T(8,128)S(1)}, f32[48,128]{1,0:T(8,128)}, u32[]{:S(2)}) copy-start(f32[48,128]{1,0:T(8,128)} %param.12) | copy-start | bytes 73732
  767.4 67.1 %copy-start.5 = (f32[48,128]{1,0:T(8,128)S(1)}, f32[48,128]{1,0:T(8,128)}, u32[]{:S(2)}) copy-start(f32[48,128]{1,0:T(8,128)} %param.13) | copy-start | bytes 73732
  768.9 12.1 %all-to-all-start = ((f32[48,2,128]{2,1,0:T(2,128)}), f32[48,2,128]{2,1,0:T(2,128)S(1)}, u32[]{:S(2)}, u32[]{:S(2)}) async-start(f32[48,2,128]{2,1,0:T(2,128)} %copy.39), calls=%async_computation.1 | async-start | bytes 98304 | tf_op jit(solution)/shard_map/all_to_all | solution.py:126
  812.1 8.9 %all-to-all-start.1 = ((f32[4,1,3072]{2,1,0:T(1,128)}), f32[4,1,3072]{2,1,0:T(1,128)S(1)}, u32[]{:S(2)}, u32[]{:S(2)}) async-start(f32[4,1,3072]{2,1,0:T(1,128)} %reshape.356), calls=%async_computation.2 | async-start | bytes 98304 | tf_op jit(solution)/shard_map/all_to_all | solution.py:150
  834.4 26.0 %copy-start.3 = (f32[48,128]{1,0:T(8,128)}, f32[48,128]{1,0:T(8,128)S(1)}, u32[]{:S(2)}) copy-start(f32[48,128]{1,0:T(8,128)S(1)} %convolution_add_fusion) | copy-start | bytes 73732
  834.6 12.3 %collective-permute-start.1 = (f32[5,48,1]{2,1,0:T(8,128)S(1)}, f32[5,48,1]{2,1,0:T(8,128)S(1)}, u32[]{:S(2)}, u32[]{:S(2)}) collective-permute-start(f32[5,48,1]{2,1,0:T(8,128)S(1)} %get-tuple-element.288), channel_id=1, source_target_pairs={{8,0},{16,8},{24,16},{0,24},{9,1},{17,9},{25,17},{1,25},{10,2},{18... | collective-permute-start | bytes 2888 | tf_op jit(solution)/shard_map/ppermute | solution.py:19
  845.4 7.4 collective-permute-start
  852.9 4.0 collective-permute-start.2
  853.0 4.0 collective-permute-start.3
Sparse Core Ops, SparseCore 0:
  11.3 36.6 reduce-scatter.1
where the time goes:
time: 873 us; the launch traced here: 867 us
  other arithmetic  307 us (35%)
  loops' own time  243 us (28%)
  local copies, waits for them, and re-layouts  218 us (25%)
  matrix products  33.7 us (4%)
  blocking collectives  19.6 us (2%)
  waiting for transfers between devices  17.1 us (2%)
  between operations  15.1 us (2%)
  starting transfers between devices  14.4 us (2%)
    dynamic_update_slice x360, other arithmetic, on_device(): lax.scan(order_advance, (order_empty, order_empty), jnp.arange(degrees, d...  252 us
    another operation x1, loops' own time, on_device(): lax.scan(order_advance, (order_empty, order_empty), jnp.arange(degrees, d...  243 us
    dynamic_slice x360, local copies, waits for them, and re-layouts, on_device(): lax.scan(order_advance, (order_empty, order_empty), jnp.arange(degrees, d...  210 us
  transfers between devices with their start and end apart: 7, of which 4 were waited for; matrix products, arithmetic and copies ran while one was open for 59% of the time, Pallas kernels for 0%

commit v1 on v0

v1 whole, which is shorter than its diff:
```python
import functools
import math

import jax
import jax.numpy as jnp
import numpy as np
from jax import lax
from jax.experimental import pallas as pl
from jax.experimental.pallas import tpu as pltpu
from jax.sharding import PartitionSpec as P

COURANT = 0.35
CHUNK = 16
F32 = jnp.float32
BF16 = jnp.bfloat16


def split(x):
    high = x.astype(BF16)
    return high, (x - high.astype(F32)).astype(BF16)


def flip_lanes(x):
    n = x.shape[1]
    i = lax.broadcasted_iota(jnp.int32, (n, n), 0)
    j = lax.broadcasted_iota(jnp.int32, (n, n), 1)
    anti = (i + j == n - 1).astype(F32)
    return jnp.dot(x, anti, precision=lax.Precision.HIGHEST, preferred_element_type=F32)


def fill_table(dims, lat_ref, picked_ref, root_ref, ratio_ref, hi_ref, lo_ref):
    gx, gy, per, sp, degrees = dims
    half = lat_ref.shape[1]
    base = (lax.axis_index("gx") * gy + lax.axis_index("gy")) * per
    orders = (base + lax.broadcasted_iota(jnp.int32, (sp, 128), 0)).astype(F32)
    squares = orders * orders
    widen = lambda x: jnp.concatenate([x] * (half // 128), axis=1)
    cosines = jnp.broadcast_to(lat_ref[0:1, :], (sp, half))
    exponent = widen(orders) * lat_ref[1:2, :] + widen(picked_ref[...])
    log_shift = jnp.clip(-exponent - 80.0, 0.0, 80.0)
    slot = lax.broadcasted_iota(jnp.int32, (sp, half), 0)
    scale = 1.0 / math.sqrt(4.0 * math.pi)
    seeds = jnp.where(slot < per, jnp.exp(exponent + log_shift) * scale, 0.0)
    unscale = jnp.exp(-log_shift)

    def block(number, carry):
        previous, before, below = carry
        for inner in range(8):
            degree = number * 8 + inner
            value = degree.astype(F32)
            gap = value * value - squares
            inverse = lax.rsqrt(jnp.maximum(gap, 1.0))
            growth = root_ref[degree] * inverse
            damping = ratio_ref[degree] * inverse * below
            stepped = (widen(growth) * cosines) * previous - widen(damping) * before
            values = jnp.where(widen(orders) == value, seeds, stepped)
            high, low = split(values * unscale)
            rows = pl.ds(pl.multiple_of(degree * sp, sp), sp)
            hi_ref[rows, :] = high
            lo_ref[rows, :] = low
            previous, before, below = values, previous, jnp.maximum(gap, 0.0) * inverse
        return previous, before, below

    empty = jnp.zeros((sp, half), F32)
    lax.fori_loop(0, degrees // 8, block, (empty, empty, jnp.zeros((sp, 128), F32)))


def transform(dims, bands, lat_ref, love_ref, hi_ref, lo_ref):
    gx, gy, per, sp, degrees = dims
    half = lat_ref.shape[1]
    base = (lax.axis_index("gx") * gy + lax.axis_index("gy")) * per
    weights = lat_ref[2:3, :]
    mirrored = flip_lanes(jnp.concatenate(bands[gy // 2 :], axis=0))
    rows = 2 * sp
    near = jnp.concatenate(bands[: gy // 2], axis=1)
    far = jnp.concatenate(
        [mirrored[b * rows : (b + 1) * rows] for b in reversed(range(gy // 2))], axis=1
    )
    folded = jnp.concatenate([(near + far) * weights, (near - far) * weights], axis=0)
    f_hi, f_lo = split(folded)
    f_both = jnp.concatenate([f_hi, f_lo], axis=0)
    total = 2 * rows
    span = CHUNK * sp
    row = lax.broadcasted_iota(jnp.int32, (total, span), 0)
    column = lax.broadcasted_iota(jnp.int32, (total, span), 1)
    slot = row % sp
    order = base + slot
    same = (slot == column % sp) & ((column // sp + order) % 2 == row // rows)
    mask = jnp.where(same, jnp.where(order == 0, 1.0, 2.0), 0.0).astype(F32)
    nt = (((1,), (1,)), ((), ()))
    nn = (((1,), (0,)), ((), ()))
    dot = functools.partial(lax.dot_general, preferred_element_type=F32)

    def chunk(number, acc):
        at = pl.ds(pl.multiple_of(number * span, span), span)
        p_hi = hi_ref[at, :]
        p_lo = lo_ref[at, :]
        wide = dot(f_both, p_hi, nt)
        spectrum = wide[:total] + wide[total:] + dot(f_hi, p_lo, nt)
        c_hi, c_lo = split(spectrum * mask * love_ref[pl.ds(number, 1), :])
        back = dot(jnp.concatenate([c_hi, c_lo], axis=0), p_hi, nn)
        return acc + (back[:total] + back[total:] + dot(c_hi, p_lo, nn))

    acc = lax.fori_loop(0, degrees // CHUNK, chunk, jnp.zeros((total, half), F32))
    north = acc[:rows] + acc[rows:]
    south = acc[:rows] - acc[rows:]
    out = [north[:, b * 128 : (b + 1) * 128] for b in range(gy // 2)]
    for b in reversed(range(gy // 2)):
        out.append(flip_lanes(south[:, b * 128 : (b + 1) * 128]))
    return out


def legendre_kernel(dims, f_ref, lat_ref, picked_ref, love_ref, root_ref, ratio_ref, g_ref, hi_ref, lo_ref):
    fill_table(dims, lat_ref, picked_ref, root_ref, ratio_ref, hi_ref, lo_ref)
    bands = [f_ref[b] for b in range(dims[1])]
    for b, out in enumerate(transform(dims, bands, lat_ref, love_ref, hi_ref, lo_ref)):
        g_ref[b] = out


def trig(orders, columns, is_sine, lon_count):
    phase = (orders * columns + is_sine * (lon_count // 4 * 3)) % lon_count
    return jnp.cos(phase.astype(F32) * (2.0 * math.pi / lon_count))


def on_device(height, east_speed, north_speed, water_depth, ocean_mask, fold_partner, love_factor):
    tile_lon, tile_lat = height.shape
    degrees = love_factor.shape[0]
    gx = lax.axis_size("gx")
    gy = lax.axis_size("gy")
    x = lax.axis_index("gx")
    y = lax.axis_index("gy")
    lon_count = tile_lon * gx
    lat_count = tile_lat * gy
    half = lat_count // 2
    per = -(-degrees // (gx * gy))
    sp = -(-per // 16) * 16
    padded = -(-degrees // CHUNK) * CHUNK
    dims = (gx, gy, per, sp, padded)
    rows = 2 * sp
    wet = ocean_mask.astype(F32)
    surface = wet * height
    is_top = y == gy - 1

    def lanes(v):
        return jnp.pad(v, ((0, 0), (0, tile_lat - v.shape[1])))

    top = lanes(jnp.stack([wet[:, -1], surface[:, -1], water_depth[:, -1], north_speed[:, -1]]))
    low = lanes(jnp.stack([wet[:, 0], surface[:, 0], water_depth[:, 0]]))
    pack = jnp.concatenate(
        [
            surface,
            wet[:1], water_depth[:1],
            wet[-1:], water_depth[-1:], east_speed[-1:],
            top[:3],
        ],
        axis=0,
    )
    gathered = lax.all_gather(pack, "gx", axis=0)

    slot_rows = jnp.arange(gy * rows, dtype=jnp.int32)
    slot = slot_rows % sp
    sine = slot_rows // sp % 2
    group_orders = (x * gy + slot_rows // rows) * per + slot
    columns = jnp.arange(lon_count, dtype=jnp.int32)
    valid = (slot < per).astype(F32)
    ahead = trig(group_orders[:, None], columns[None, :], sine[:, None], lon_count) * valid[:, None]
    ext = tile_lon + 8
    place = jnp.arange(gx * ext, dtype=jnp.int32)
    within = place % ext
    offset = jnp.where(within <= tile_lon, within, jnp.where(within == tile_lon + 1, -1, 0))
    ext_columns = (place // ext * tile_lon + offset + lon_count) % lon_count
    behind = trig(group_orders[None, :], ext_columns[:, None], sine[None, :], lon_count) * valid[None, :]

    band_rows = jnp.dot(
        ahead, gathered[:, :tile_lon].reshape(lon_count, tile_lat),
        precision=lax.Precision.HIGH, preferred_element_type=F32,
    ).reshape(gy, rows, tile_lat)
    edges = jnp.concatenate([top, low, jnp.zeros((1, tile_lat), F32)], axis=0)
    sent = jnp.concatenate([band_rows, jnp.broadcast_to(edges, (gy,) + edges.shape)], axis=1)
    came = lax.all_to_all(sent, "gy", split_axis=0, concat_axis=0, tiled=True)

    theta = np.pi * (np.arange(half) + 0.5) / lat_count
    quadrature = np.pi / lat_count * (2.0 * np.pi / lon_count) * np.sin(theta)
    lat_table = np.zeros((8, half), np.float32)
    lat_table[0], lat_table[1], lat_table[2] = np.cos(theta), np.log(np.sin(theta)), quadrature
    slots = per * gx * gy + sp
    k = np.arange(1, slots, dtype=np.float64)
    logs = np.concatenate([[0.0], np.cumsum(0.5 * np.log((2.0 * k + 1.0) / (2.0 * k)))])
    first = (x * gy + y) * per
    picked = lax.dynamic_slice(jnp.asarray(logs.astype(np.float32)), (first,), (sp,))
    picked = jnp.broadcast_to(picked[:, None], (sp, 128))
    ell = np.arange(padded, dtype=np.float64)
    root = np.sqrt(np.maximum(4.0 * ell * ell - 1.0, 1.0))
    ratio = root / np.sqrt(np.maximum(4.0 * (ell - 1.0) ** 2 - 1.0, 1.0))
    love = jnp.repeat(jnp.pad(love_factor, (0, padded - degrees)), sp).reshape(padded // CHUNK, CHUNK * sp)

    vmem = pl.BlockSpec(memory_space=pltpu.VMEM)
    smem = pl.BlockSpec(memory_space=pltpu.SMEM)
    grid_rows = pl.pallas_call(
        functools.partial(legendre_kernel, dims),
        out_shape=jax.ShapeDtypeStruct((gy, rows, tile_lat), F32),
        in_specs=[vmem, vmem, vmem, vmem, smem, smem],
        out_specs=vmem,
        scratch_shapes=[
            pltpu.VMEM((padded * sp, half), BF16),
            pltpu.VMEM((padded * sp, half), BF16),
        ],
        compiler_params=pltpu.CompilerParams(vmem_limit_bytes=40 * 2**20),
    )(
        came[:, :rows], jnp.asarray(lat_table), picked, love,
        jnp.asarray(root.astype(np.float32)), jnp.asarray(ratio.astype(np.float32)),
    )
    norths = jnp.concatenate([grid_rows[1:, :, :1], jnp.zeros((1, rows, 1), F32)], axis=0)
    souths = jnp.concatenate([jnp.zeros((1, rows, 1), F32), grid_rows[:-1, :, -1:]], axis=0)
    rims = jnp.concatenate([norths, souths], axis=2)
    rims = jnp.pad(jnp.swapaxes(rims, 1, 2), ((0, 0), (0, 6), (0, tile_lat - rows)))
    back = lax.all_to_all(
        jnp.concatenate([grid_rows, rims], axis=1), "gy", split_axis=0, concat_axis=0, tiled=True
    )
    terms = back[:, :rows].reshape(gy * rows, tile_lat)
    rim_terms = jnp.swapaxes(back[:, rows : rows + 2, :rows], 1, 2).reshape(gy * rows, 2)
    made = jnp.dot(
        behind, jnp.concatenate([terms, rim_terms], axis=1),
        precision=lax.Precision.HIGH, preferred_element_type=F32,
    ).reshape(gx, ext, tile_lat + 2)
    folded = made[:, :tile_lon, tile_lat - 1][fold_partner][:, ::-1]
    north_rim = jnp.where(is_top, folded, made[:, :tile_lon, tile_lat])
    south_rim = made[:, :tile_lon, tile_lat + 1]
    rim = jnp.stack([north_rim, south_rim], axis=1)
    rim = jnp.pad(rim, ((0, 0), (0, 6), (0, tile_lat - tile_lon)))
    parts = lax.all_to_all(
        jnp.concatenate([made[:, :, :tile_lat], rim], axis=1), "gx", split_axis=0, concat_axis=0, tiled=True
    )
    sal_all = jnp.sum(parts.reshape(gx, ext + 8, tile_lat), axis=0)
    sal = sal_all[:tile_lon]

    east_of = lax.dynamic_index_in_dim(gathered, (x + 1) % gx, 0, False)
    west_of = lax.dynamic_index_in_dim(gathered, (x + gx - 1) % gx, 0, False)
    fold_of = lax.dynamic_index_in_dim(gathered, fold_partner[x], 0, False)[tile_lon + 5 :, :tile_lon][:, ::-1]
    north_of = came[jnp.minimum(y + 1, gy - 1), rows + 4 : rows + 7, :tile_lon]
    north_of = jnp.where(is_top, fold_of, north_of)
    south_of = came[jnp.maximum(y - 1, 0), rows : rows + 4, :tile_lon]

    pressure = surface - sal
    east_p = east_of[:1] - sal_all[tile_lon : tile_lon + 1]
    west_p = west_of[tile_lon - 1 : tile_lon] - sal_all[tile_lon + 1 : tile_lon + 2]
    north_p = north_of[1] - sal_all[ext, :tile_lon]
    south_p = south_of[1] - sal_all[ext + 1, :tile_lon]

    cat = functools.partial(jnp.concatenate, axis=0)
    p_x = cat([west_p, pressure, east_p])
    w_x = cat([west_of[tile_lon + 2 : tile_lon + 3], wet, east_of[tile_lon : tile_lon + 1]])
    d_x = cat([west_of[tile_lon + 3 : tile_lon + 4], water_depth, east_of[tile_lon + 1 : tile_lon + 2]])
    u_x = cat([west_of[tile_lon + 4 : tile_lon + 5], east_speed])
    east = w_x[:-1] * w_x[1:] * (u_x - COURANT * (p_x[1:] - p_x[:-1]))
    east_flux = 0.5 * (d_x[:-1] + d_x[1:]) * east
    cat = lambda parts: jnp.concatenate(parts, axis=1)
    p_y = cat([south_p[:, None], pressure, north_p[:, None]])
    w_y = cat([south_of[0][:, None], wet, north_of[0][:, None]])
    d_y = cat([south_of[2][:, None], water_depth, north_of[2][:, None]])
    v_y = cat([south_of[3][:, None], north_speed])
    north = w_y[:, :-1] * w_y[:, 1:] * (v_y - COURANT * (p_y[:, 1:] - p_y[:, :-1]))
    north_flux = 0.5 * (d_y[:, :-1] + d_y[:, 1:]) * north
    gate = jnp.where(y > 0, 1.0, 0.0).astype(F32)
    south_flux = cat([north_flux[:, :1] * gate, north_flux[:, 1:-1]])
    height_next = wet * (
        surface - COURANT * (east_flux[1:] - east_flux[:-1] + north_flux[:, 1:] - south_flux)
    )
    return sal, east[1:], north[:, 1:], height_next


def solution(mesh):
    spec = P("gx", "gy")
    return jax.shard_map(
        on_device, mesh=mesh, in_specs=(spec,) * 5 + (P(), P()), out_specs=(spec,) * 4, check_vma=False
    )
```

time: 873 us -> 73.5 us (0.08)
  other arithmetic: 307 us -> 2.22 us
  loops' own time: 243 us -> 0 us
  local copies, waits for them, and re-layouts: 218 us -> 13.9 us
  matrix products: 33.7 us -> 2.55 us
  Pallas kernels: 0 us -> 14.3 us
  between operations: 15.1 us -> 3.04 us
  blocking collectives: 19.6 us -> 10.8 us
    dynamic_update_slice x360 -> x0, other arithmetic: 252 us -> none  [on_device(): lax.scan(order_advance, (order_empty, order_empty), jnp.arange(degrees, d...]
    another operation x1 -> x0, loops' own time: 243 us -> none  [on_device(): lax.scan(order_advance, (order_empty, order_empty), jnp.arange(degrees, d...]
    dynamic_slice x362 -> x5, local copies, waits for them, and re-layouts: 210 us -> 1.45 us  [the longest x1 0.76 us: on_device(): lax.dynamic_slice(jnp.asarray(logs.astype(np.float32)), (first,), (sp,))]
    dot_general x6 -> x2, matrix products: 33.7 us -> 2.55 us  [the longest x1 1.32 us: on_device(): jnp.dot(ahead, gathered[:, :tile_lon].reshape(lon_count, tile_lat), preci...]
    cos x360 -> x0, other arithmetic: 15.7 us -> none  [latitude_rows(): return (jnp.cos(colatitude), sines, quadrature)]
    pallas_call x0 -> x1, Pallas kernels: none -> 14.3 us  [on_device(): pl.pallas_call(functools.partial(legendre_kernel, dims), out_shape=jax.Sh...]
    sqrt x360 -> x0, other arithmetic: 13.6 us -> none  [legendre_next(): jnp.sqrt(jnp.maximum(below_value * below_value - orders * orders, 0.0) /...]
    mul x7 -> x5, other arithmetic: 12.7 us -> 0.31 us  [the longest x1 0.14 us: on_device(): east_flux = 0.5 * (d_x[:-1] + d_x[1:]) * east]
  transfers between devices with their start and end apart: 7 -> 3, of which waited for: 4 -> 2; matrix products, arithmetic and copies ran while one was open for 59% -> 4% of each run, Pallas kernels for 0% -> 0%
where the time goes in v1:
time: 73.5 us; the launch traced here: 72.7 us
  Pallas kernels  14.3 us (19%)
  local copies, waits for them, and re-layouts  13.9 us (19%)
  starting transfers between devices  13.4 us (18%)
  waiting for transfers between devices  12.5 us (17%)
  blocking collectives  10.8 us (15%)
  between operations  3.04 us (4%)
  matrix products  2.55 us (3%)
  other arithmetic  2.22 us (3%)
    pallas_call x1, Pallas kernels, on_device(): pl.pallas_call(functools.partial(legendre_kernel, dims), out_shape=jax.Sh...  14.3 us
    all_gather x1, blocking collectives, on_device(): gathered = lax.all_gather(pack, 'gx', axis=0)  10.8 us
    unnamed x34, local copies, waits for them, and re-layouts  8.16 us
    all_to_all x1, waiting for transfers between devices, on_device(): lax.all_to_all(jnp.concatenate([made[:, :, :tile_lat], rim], axis=1), 'gx...  6.72 us
    all_to_all x1, waiting for transfers between devices, on_device(): lax.all_to_all(jnp.concatenate([grid_rows, rims], axis=1), 'gy', split_ax...  5.78 us
    all_to_all x1, starting transfers between devices, on_device(): lax.all_to_all(jnp.concatenate([grid_rows, rims], axis=1), 'gy', split_ax...  5.09 us
    all_to_all x1, starting transfers between devices, on_device(): came = lax.all_to_all(sent, 'gy', split_axis=0, concat_axis=0, tiled=True)  4.87 us
    all_to_all x1, starting transfers between devices, on_device(): lax.all_to_all(jnp.concatenate([made[:, :, :tile_lat], rim], axis=1), 'gx...  3.41 us
  transfers between devices with their start and end apart: 3, of which 2 were waited for; matrix products, arithmetic and copies ran while one was open for 4% of the time, Pallas kernels for 0%

profile of v1, /device:TPU:0, one launch (start us, length us, event | category | flops | bytes accessed | tf_op | source)
XLA Modules:
  0.0 72.7 jit_solution(4133196442119167319)
XLA Ops:
  0.6 0.8 %copy.159 = s32[48,128]{0,1:T(8,128)S(1)} copy(s32[48,128]{1,0:T(8,128)} %param.15) | data formatting | bytes 49152 | tf_op args[4]
  1.8 0.7 copy-done.3
  3.5 0.7 copy-done.7
  4.2 10.8 %all-gather = f32[448,128]{1,0:T(8,128)S(1)} all-gather(f32[56,128]{1,0:T(8,128)S(1)} %concatenate.78), channel_id=2, replica_groups=mesh['gy'=4,'gx'=8] {'gx'}, dimensions={0}, use_global_device_ids=true | all-gather | bytes 258048 | tf_op jit(solution)/shard_map/all_gather | solution.py:158
  15.2 1.3 %fusion.15 = f32[4,32,128]{2,1,0:T(8,128)S(1)} fusion(f32[384,128,1]{1,0,2:T(8,128)S(1)} %bitcast.78, f32[4,32]{1,0:T(4,128)S(1)} %compare_convert_fusion, s32[4,32]{1,0:T(4,128)S(1)} %get-tuple-element.58, s32[4,32]{1,0:T(4,128)S(1)} %get-tuple-element.57), kind=kOutput, calls=%fused_computation.19 | convolution fusion | flops 38289408 | bytes 263680 | tf_op jit(solution)/shard_map/dot_general | solution.py:174
  16.6 0.6 pad_maximum_fusion
  17.2 4.9 %all-to-all-start = ((f32[4,40,128]{2,1,0:T(8,128)}), f32[4,40,128]{2,1,0:T(8,128)S(1)}, u32[]{:S(2)}, u32[]{:S(2)}) async-start(f32[4,40,128]{2,1,0:T(8,128)} %pad_maximum_fusion), calls=%async_computation | async-start | bytes 163840 | tf_op jit(solution)/shard_map/all_to_all | solution.py:180
  22.1 0.6 copy-done.9
  22.7 0.6 dynamic_slice.26
  25.6 0.7 copy-done.8
  27.6 0.8 %dynamic_slice.22 = f32[16]{0:T(128)S(1)} dynamic-slice(f32[400]{0:T(512)} %constant.193.clone, s32[]{:T(128)S(6)} %select_n.206), dynamic_slice_sizes={16} | dynamic-slice | bytes 132 | tf_op jit(solution)/shard_map/dynamic_slice | solution.py:190
  28.5 0.6 copy-done.1
  29.1 14.3 %shard_map.138 = f32[4,32,128]{2,1,0:T(8,128)S(1)} custom-call(f32[4,32,128]{2,1,0:T(8,128)S(1)} %slice.265.f_ref, f32[8,256]{1,0:T(8,128)S(1)} %copy-done, f32[16,128]{1,0:T(8,128)S(1)} %broadcast_in_dim.20.picked_ref, f32[23,256]{1,0:T(8,128)S(1)} %broadcast_in_dim.41.love_ref, f32[368]{0:T(512)S(1)} %copy-done.1, f32[368]{0:T(512)S(1)} %copy-done.2), custom_call_target="tpu_custom_call" | custom-call | tf_op jit(solution)/shard_map/pallas_call | solution.py:199
  43.7 0.6 select_maximum_fusion.1
  44.3 5.1 %all-to-all-start.1 = ((f32[4,40,128]{2,1,0:T(8,128)}), f32[4,40,128]{2,1,0:T(8,128)S(1)}, u32[]{:S(2)}, u32[]{:S(2)}) async-start(f32[4,40,128]{2,1,0:T(8,128)} %select_maximum_fusion.1), calls=%async_computation.1 | async-start | bytes 163840 | tf_op jit(solution)/shard_map/all_to_all | solution.py:217
  49.4 5.8 %all-to-all-done.1 = f32[4,40,128]{2,1,0:T(8,128)S(1)} async-done(((f32[4,40,128]{2,1,0:T(8,128)}), f32[4,40,128]{2,1,0:T(8,128)S(1)}, u32[]{:S(2)}, u32[]{:S(2)}) %all-to-all-start.1) | async-done | bytes 81952 | tf_op jit(solution)/shard_map/all_to_all | solution.py:217
  55.3 1.2 %fusion.4 = f32[448,130]{0,1:T(8,128)S(1)} fusion(f32[128,2]{1,0:T(8,128)S(1)} %bitcast.80, f32[128,128]{1,0:T(8,128)S(1)} %bitcast.81, f32[128]{0:T(128)S(1)} %compare_convert_fusion.1, s32[128]{0:T(128)S(1)} %get-tuple-element.60, s32[448]{0:T(512)S(1)} %add_select_fusion.6, s32[128]{0:T(128)S(1)} %get-tuple-element.59), kind=kOutput, calls=%fused_computation.9 | convolution fusion | flops 45375744 | bytes 302848 | tf_op jit(solution)/shard_map/dot_general | solution.py:222
  56.9 0.6 gather_fusion
  57.8 0.9 %copy.169 = f32[8,64,128]{2,1,0:T(8,128)} copy(f32[8,64,128]{1,0,2:T(8,128)S(1)} %select_maximum_fusion) | data formatting | bytes 524288 | tf_op jit(solution)/shard_map/concatenate | solution.py:232
  58.7 3.4 %all-to-all-start.2 = ((f32[8,64,128]{2,1,0:T(8,128)}), f32[8,64,128]{2,1,0:T(8,128)S(1)}, u32[]{:S(2)}, u32[]{:S(2)}) async-start(f32[8,64,128]{2,1,0:T(8,128)} %copy.169), calls=%async_computation.2 | async-start | bytes 524288 | tf_op jit(solution)/shard_map/all_to_all | solution.py:231
  62.3 6.7 %all-to-all-done.2 = f32[8,64,128]{2,1,0:T(8,128)S(1)} async-done(((f32[8,64,128]{2,1,0:T(8,128)}), f32[8,64,128]{2,1,0:T(8,128)S(1)}, u32[]{:S(2)}, u32[]{:S(2)}) %all-to-all-start.2) | async-done | bytes 262176 | tf_op jit(solution)/shard_map/all_to_all | solution.py:231
  70.5 0.7 copy.186
  71.2 0.7 copy.185
  72.0 0.7 copy.184
  (104 shorter events, 5.9 us)
Async XLA Ops:
  0.6 0.9 %copy-start.6 = (f32[48,128]{1,0:T(8,128)S(1)}, f32[48,128]{1,0:T(8,128)}, u32[]{:S(2)}) copy-start(f32[48,128]{1,0:T(8,128)} %param.11) | copy-start | bytes 73732
  1.7 0.7 %copy-start.3 = (f32[48,128]{1,0:T(8,128)S(1)}, f32[48,128]{1,0:T(8,128)}, u32[]{:S(2)}) copy-start(f32[48,128]{1,0:T(8,128)} %param.14) | copy-start | bytes 73732
  2.5 0.7 %copy-start.4 = (f32[48,128]{1,0:T(8,128)S(1)}, f32[48,128]{1,0:T(8,128)}, u32[]{:S(2)}) copy-start(f32[48,128]{1,0:T(8,128)} %param.13) | copy-start | bytes 73732
  3.4 0.8 %copy-start.7 = (f32[48,128]{1,0:T(8,128)S(1)}, f32[48,128]{1,0:T(8,128)}, u32[]{:S(2)}) copy-start(f32[48,128]{1,0:T(8,128)} %param.12) | copy-start | bytes 73732
  17.2 11.2 %all-to-all-start = ((f32[4,40,128]{2,1,0:T(8,128)}), f32[4,40,128]{2,1,0:T(8,128)S(1)}, u32[]{:S(2)}, u32[]{:S(2)}) async-start(f32[4,40,128]{2,1,0:T(8,128)} %pad_maximum_fusion), calls=%async_computation | async-start | bytes 163840 | tf_op jit(solution)/shard_map/all_to_all | solution.py:180
  22.1 0.7 copy-start.9
  25.6 0.7 copy-start.8
  28.4 0.7 copy-start.1
  28.4 0.7 copy-start.2
  28.4 0.7 copy-start
  44.3 10.9 %all-to-all-start.1 = ((f32[4,40,128]{2,1,0:T(8,128)}), f32[4,40,128]{2,1,0:T(8,128)S(1)}, u32[]{:S(2)}, u32[]{:S(2)}) async-start(f32[4,40,128]{2,1,0:T(8,128)} %select_maximum_fusion.1), calls=%async_computation.1 | async-start | bytes 163840 | tf_op jit(solution)/shard_map/all_to_all | solution.py:217
  58.7 10.3 %all-to-all-start.2 = ((f32[8,64,128]{2,1,0:T(8,128)}), f32[8,64,128]{2,1,0:T(8,128)S(1)}, u32[]{:S(2)}, u32[]{:S(2)}) async-start(f32[8,64,128]{2,1,0:T(8,128)} %copy.169), calls=%async_computation.2 | async-start | bytes 524288 | tf_op jit(solution)/shard_map/all_to_all | solution.py:231
  69.1 0.6 copy-start.5

commit v2 on v1

v2 whole, which is shorter than its diff:
```python
import functools
import math

import jax
import jax.numpy as jnp
import numpy as np
from jax import lax
from jax.experimental import pallas as pl
from jax.experimental.pallas import tpu as pltpu
from jax.sharding import PartitionSpec as P

COURANT = 0.35
CHUNK = 16
F32 = jnp.float32
BF16 = jnp.bfloat16


def split(x):
    high = x.astype(BF16)
    return high, (x - high.astype(F32)).astype(BF16)


def flip_lanes(x):
    n = x.shape[1]
    i = lax.broadcasted_iota(jnp.int32, (n, n), 0)
    j = lax.broadcasted_iota(jnp.int32, (n, n), 1)
    anti = (i + j == n - 1).astype(F32)
    return jnp.dot(x, anti, precision=lax.Precision.HIGHEST, preferred_element_type=F32)


def fill_table(dims, lat_ref, logs_ref, root_ref, ratio_ref, hi_ref, lo_ref):
    gx, gy, per, sp, degrees = dims
    half = lat_ref.shape[1]
    base = (lax.axis_index("gx") * gy + lax.axis_index("gy")) * per
    orders = (base + lax.broadcasted_iota(jnp.int32, (sp, 128), 0)).astype(F32)
    squares = orders * orders
    widen = lambda x: jnp.concatenate([x] * (half // 128), axis=1)
    cosines = jnp.broadcast_to(lat_ref[0:1, :], (sp, half))
    slot_row = lax.broadcasted_iota(jnp.int32, (sp, 128), 0)
    picked = jnp.zeros((sp, 128), F32)
    for s in range(per):
        picked = jnp.where(slot_row == s, logs_ref[base + s], picked)
    exponent = widen(orders) * lat_ref[1:2, :] + widen(picked)
    log_shift = jnp.clip(-exponent - 80.0, 0.0, 80.0)
    slot = lax.broadcasted_iota(jnp.int32, (sp, half), 0)
    scale = 1.0 / math.sqrt(4.0 * math.pi)
    seeds = jnp.where(slot < per, jnp.exp(exponent + log_shift) * scale, 0.0)
    unscale = jnp.exp(-log_shift)

    def block(number, carry):
        previous, before, below = carry
        for inner in range(8):
            degree = number * 8 + inner
            value = degree.astype(F32)
            gap = value * value - squares
            inverse = lax.rsqrt(jnp.maximum(gap, 1.0))
            growth = root_ref[degree] * inverse
            damping = ratio_ref[degree] * inverse * below
            stepped = (widen(growth) * cosines) * previous - widen(damping) * before
            values = jnp.where(widen(orders) == value, seeds, stepped)
            high, low = split(values * unscale)
            rows = pl.ds(pl.multiple_of(degree * sp, sp), sp)
            hi_ref[rows, :] = high
            lo_ref[rows, :] = low
            previous, before, below = values, previous, jnp.maximum(gap, 0.0) * inverse
        return previous, before, below

    empty = jnp.zeros((sp, half), F32)
    start = (empty, empty, jnp.zeros((sp, 128), F32))
    return lambda first, last, carry=start: lax.fori_loop(first, last, block, carry)


def transform(dims, bands, lat_ref, love_ref, hi_ref, lo_ref):
    known = love_ref.shape[0]
    gx, gy, per, sp, degrees = dims
    half = lat_ref.shape[1]
    base = (lax.axis_index("gx") * gy + lax.axis_index("gy")) * per
    weights = lat_ref[2:3, :]
    mirrored = flip_lanes(jnp.concatenate(bands[gy // 2 :], axis=0))
    rows = 2 * sp
    near = jnp.concatenate(bands[: gy // 2], axis=1)
    far = jnp.concatenate(
        [mirrored[b * rows : (b + 1) * rows] for b in reversed(range(gy // 2))], axis=1
    )
    folded = jnp.concatenate([(near + far) * weights, (near - far) * weights], axis=0)
    f_hi, f_lo = split(folded)
    f_both = jnp.concatenate([f_hi, f_lo], axis=0)
    total = 2 * rows
    span = CHUNK * sp
    row = lax.broadcasted_iota(jnp.int32, (total, span), 0)
    column = lax.broadcasted_iota(jnp.int32, (total, span), 1)
    slot = row % sp
    order = base + slot
    same = (slot == column % sp) & ((column // sp + order) % 2 == row // rows)
    mask = jnp.where(same, jnp.where(order == 0, 1.0, 2.0), 0.0).astype(F32)
    nt = (((1,), (1,)), ((), ()))
    nn = (((1,), (0,)), ((), ()))
    dot = functools.partial(lax.dot_general, preferred_element_type=F32)

    lane = lax.broadcasted_iota(jnp.int32, (1, span), 1)

    def chunk(number, acc):
        love = jnp.zeros((1, span), F32)
        for k in range(CHUNK):
            degree = number * CHUNK + k
            factor = love_ref[jnp.minimum(degree, known - 1)] * (degree < known).astype(F32)
            love = jnp.where(lane // sp == k, factor, love)
        at = pl.ds(pl.multiple_of(number * span, span), span)
        p_hi = hi_ref[at, :]
        p_lo = lo_ref[at, :]
        wide = dot(f_both, p_hi, nt)
        spectrum = wide[:total] + wide[total:] + dot(f_hi, p_lo, nt)
        c_hi, c_lo = split(spectrum * mask * love)
        back = dot(jnp.concatenate([c_hi, c_lo], axis=0), p_hi, nn)
        return acc + (back[:total] + back[total:] + dot(c_hi, p_lo, nn))

    acc = lax.fori_loop(0, degrees // CHUNK, chunk, jnp.zeros((total, half), F32))
    north = acc[:rows] + acc[rows:]
    south = acc[:rows] - acc[rows:]
    out = [north[:, b * 128 : (b + 1) * 128] for b in range(gy // 2)]
    for b in reversed(range(gy // 2)):
        out.append(flip_lanes(south[:, b * 128 : (b + 1) * 128]))
    return out


def wave(product, lon_count):
    lon = float(lon_count)
    phase = product - lon * jnp.floor((product + 0.5) * (1.0 / lon))
    y = jnp.abs(phase - lon / 2)
    z = jnp.minimum(y, lon / 2 - y) * (2.0 * math.pi / lon)
    q = z * z
    series = jnp.full_like(q, 1.0 / math.factorial(12))
    for k in (10, 8, 6, 4, 2, 0):
        series = series * q + (-1.0) ** (k // 2) / math.factorial(k)
    return jnp.where(y < lon / 4, -series, series)


def group_slots(dims, shape, axis):
    gx, gy, per, sp, degrees = dims
    index = lax.broadcasted_iota(jnp.int32, shape, axis)
    slot = index % sp
    orders = (lax.axis_index("gx") * gy + index // (2 * sp)) * per + slot
    return orders.astype(F32), (index // sp % 2).astype(F32), (slot < per).astype(F32)


def trig_ahead(dims, lon_count):
    rows = dims[1] * 2 * dims[3]
    orders, sine, valid = group_slots(dims, (rows, 128), 0)
    lane = lax.broadcasted_iota(jnp.int32, (rows, 128), 1)
    blocks = []
    for n in range(lon_count // 128):
        product = orders * (lane + 128 * n).astype(F32) + sine * (0.75 * lon_count)
        blocks.append(wave(product, lon_count) * valid)
    return jnp.concatenate(blocks, axis=1)


def trig_behind(dims, tile_lon, lon_count):
    rows = dims[1] * 2 * dims[3]
    ext = tile_lon + 8
    orders, sine, valid = group_slots(dims, (ext, rows), 1)
    within = lax.broadcasted_iota(jnp.int32, (ext, rows), 0)
    blocks = []
    for t in range(dims[0]):
        column = t * tile_lon + within
        after = (t + 1) * tile_lon % lon_count
        prior = (t * tile_lon - 1) % lon_count
        column = jnp.where(within < tile_lon, column, jnp.where(within == tile_lon, after, prior))
        blocks.append(wave(orders * column.astype(F32) + sine * (0.75 * lon_count), lon_count) * valid)
    return jnp.concatenate(blocks, axis=0)


def three_pass(left, right):
    l_hi, l_lo = split(left)
    r_hi, r_lo = split(right)
    dot = functools.partial(jnp.dot, preferred_element_type=F32)
    return dot(l_hi, r_hi) + dot(l_lo, r_hi) + dot(l_hi, r_lo)


def as_row(column, reverse=False):
    n = column.shape[0]
    i = lax.broadcasted_iota(jnp.int32, (n, 128), 0)
    j = lax.broadcasted_iota(jnp.int32, (n, 128), 1)
    chosen = (j == n - 1 - i) if reverse else (i == j)
    return jnp.sum(jnp.where(chosen, column, 0.0), axis=0, keepdims=True)


def as_column(row, n, reverse=False):
    i = lax.broadcasted_iota(jnp.int32, (n, 128), 0)
    j = lax.broadcasted_iota(jnp.int32, (n, 128), 1)
    chosen = (j == n - 1 - i) if reverse else (i == j)
    return jnp.sum(jnp.where(chosen, row, 0.0), axis=1, keepdims=True)


def step_kernel(
    dims, height_hbm, east_hbm, north_hbm, depth_hbm, mask_hbm, lat_ref,
    fold_ref, love_ref, logs_ref, root_ref, ratio_ref,
    sal_ref, east_out, north_out, next_out,
    height_ref, east_ref, north_ref, depth_ref, mask_ref,
    hi_ref, lo_ref, send1, recv1, send2, recv2, send3, recv3, send4, recv4, made_ref,
    load_sem, s1, r1, s2, r2, s3, r3, s4, r4,
):
    gx, gy, per, sp, degrees = dims
    tile_lon, tile_lat = height_ref.shape
    lon_count = gx * tile_lon
    rows = 2 * sp
    ext = tile_lon + 8
    x = lax.axis_index("gx")
    y = lax.axis_index("gy")
    loads = [
        pltpu.make_async_copy(src, dst, load_sem.at[i])
        for i, (src, dst) in enumerate(
            [
                (height_hbm, height_ref), (mask_hbm, mask_ref), (depth_hbm, depth_ref),
                (east_hbm, east_ref), (north_hbm, north_ref),
            ]
        )
    ]
    for load in loads:
        load.start()
    barrier = pltpu.get_barrier_semaphore()
    for d in range(1, gx):
        pl.semaphore_signal(barrier, 1, device_id={"gx": (x + d) % gx}, device_id_type=pl.DeviceIdType.MESH)
    for d in range(1, gy):
        pl.semaphore_signal(barrier, 1, device_id={"gy": (y + d) % gy}, device_id_type=pl.DeviceIdType.MESH)
    for load in loads:
        load.wait()

    def copies(axis, here, size, source, landing, s_sem, r_sem):
        made = []
        for d in range(1, size):
            peer = (here + d) % size
            made.append(
                pltpu.make_async_remote_copy(
                    src_ref=source(peer), dst_ref=landing.at[here], send_sem=s_sem.at[peer],
                    recv_sem=r_sem.at[here], device_id={axis: peer},
                    device_id_type=pl.DeviceIdType.MESH,
                )
            )
        return made

    def arrive(axis, here, size, source, landing, s_sem, r_sem):
        for d in range(1, size):
            peer = (here + d) % size
            pltpu.make_async_remote_copy(
                src_ref=source(peer), dst_ref=landing.at[peer], send_sem=s_sem.at[peer],
                recv_sem=r_sem.at[peer], device_id={axis: peer},
                device_id_type=pl.DeviceIdType.MESH,
            ).wait_recv()

    wet = mask_ref[...].astype(F32)
    surface = wet * height_ref[...]
    depth = depth_ref[...]
    east_speed = east_ref[...]
    north_speed = north_ref[...]
    last = slice(tile_lat - 1, tile_lat)
    top = [as_row(v[:, last]) for v in (wet, surface, depth, north_speed)]
    low = [as_row(v[:, :1]) for v in (wet, surface, depth)]
    end = slice(tile_lon - 1, tile_lon)
    pack = jnp.concatenate(
        [surface, wet[:1], depth[:1], wet[end], depth[end], east_speed[end]] + top[:3], axis=0
    )
    send1[...] = pack
    recv1[x] = pack
    pl.semaphore_wait(barrier, gx + gy - 2)
    way1 = ("gx", x, gx, lambda peer: send1, recv1, s1, r1)
    out1 = copies(*way1)
    for c in out1:
        c.start()
    ahead = trig_ahead(dims, lon_count)
    fill = fill_table(dims, lat_ref, logs_ref, root_ref, ratio_ref, hi_ref, lo_ref)
    blocks = degrees // 8
    carry = fill(0, blocks // 3)
    arrive(*way1)
    every = jnp.concatenate([recv1[t, :tile_lon, :] for t in range(gx)], axis=0)
    band = three_pass(ahead, every)
    edges = jnp.concatenate(top + low + [jnp.zeros((1, tile_lat), F32)], axis=0)
    for k in range(gy):
        send2[k] = jnp.concatenate([band[k * rows : (k + 1) * rows], edges], axis=0)
    way2 = ("gy", y, gy, lambda peer: send2.at[peer], recv2, s2, r2)
    out2 = copies(*way2)
    for c in out2:
        c.start()
    recv2[y] = send2[y]
    fill(blocks // 3, blocks, carry)
    arrive(*way2)
    bands = [recv2[k, :rows, :] for k in range(gy)]
    grids = transform(dims, bands, lat_ref, love_ref, hi_ref, lo_ref)
    none = jnp.zeros((1, tile_lat), F32)
    for k in range(gy):
        north_rim = as_row(grids[k + 1][:, :1]) if k + 1 < gy else none
        south_rim = as_row(grids[k - 1][:, last]) if k > 0 else none
        rims = jnp.concatenate([north_rim, south_rim, jnp.zeros((6, tile_lat), F32)], axis=0)
        send3[k] = jnp.concatenate([grids[k], rims], axis=0)
    way3 = ("gy", y, gy, lambda peer: send3.at[peer], recv3, s3, r3)
    out3 = copies(*way3)
    for c in out3:
        c.start()
    recv3[y] = send3[y]
    behind = trig_behind(dims, tile_lon, lon_count)
    arrive(*way3)
    lane = lax.broadcasted_iota(jnp.int32, (rows, 128), 1)
    terms = []
    for k in range(gy):
        north_rim = as_column(recv3[k, rows : rows + 1, :], rows)
        south_rim = as_column(recv3[k, rows + 1 : rows + 2, :], rows)
        rim = jnp.where(lane == 0, north_rim, jnp.where(lane == 1, south_rim, 0.0))
        terms.append(jnp.concatenate([recv3[k, :rows, :], rim], axis=1))
    made = three_pass(behind, jnp.concatenate(terms, axis=0))
    for t in range(gx):
        made_ref[t] = made[t * ext : (t + 1) * ext]
    is_top = y == gy - 1
    for t in range(gx):
        piece = made[t * ext : (t + 1) * ext]
        over = made_ref[fold_ref[t]]
        folded = as_row(over[:tile_lon, last], True)
        straight = as_row(piece[:tile_lon, tile_lat : tile_lat + 1])
        south_rim = as_row(piece[:tile_lon, tile_lat + 1 : tile_lat + 2])
        north_rim = jnp.where(is_top, folded, straight)
        rims = jnp.concatenate([north_rim, south_rim, jnp.zeros((6, tile_lat), F32)], axis=0)
        send4[t] = jnp.concatenate([piece[:, :tile_lat], rims], axis=0)
    way4 = ("gx", x, gx, lambda peer: send4.at[peer], recv4, s4, r4)
    out4 = copies(*way4)
    for c in out4:
        c.start()
    recv4[x] = send4[x]

    east_of = recv1[(x + 1) % gx]
    west_of = recv1[(x + gx - 1) % gx]
    fold_of = recv1[fold_ref[x]]
    north_of = recv2[jnp.minimum(y + 1, gy - 1), rows : rows + 8, :]
    south_of = recv2[jnp.maximum(y - 1, 0), rows : rows + 8, :]

    def north_column(i):
        across = as_column(fold_of[tile_lon + 5 + i : tile_lon + 6 + i], tile_lon, True)
        return jnp.where(is_top, across, as_column(north_of[4 + i : 5 + i], tile_lon))

    n_wet, n_surface, n_depth = [north_column(i) for i in range(3)]
    s_wet, s_surface, s_depth, s_speed = [as_column(south_of[i : i + 1], tile_lon) for i in range(4)]
    rows_cat = lambda parts: jnp.concatenate(parts, axis=0)
    lanes_cat = lambda parts: jnp.concatenate(parts, axis=1)
    at = lambda block, i: block[i : i + 1]
    w_east = rows_cat([wet[1:], at(east_of, tile_lon)])
    d_east = rows_cat([depth[1:], at(east_of, tile_lon + 1)])
    w_west = at(west_of, tile_lon + 2)
    d_west = at(west_of, tile_lon + 3)
    u_west = at(west_of, tile_lon + 4)
    w_north = lanes_cat([wet[:, 1:], n_wet])
    d_north = lanes_cat([depth[:, 1:], n_depth])
    arrive(*way4)
    total = recv4[0]
    for t in range(1, gx):
        total = total + recv4[t]
    sal = total[:tile_lon]
    sal_ref[...] = sal
    pressure = surface - sal
    p_east = at(east_of, 0) - at(total, tile_lon)
    p_west = at(west_of, tile_lon - 1) - at(total, tile_lon + 1)
    p_north = n_surface - as_column(at(total, ext), tile_lon)
    p_south = s_surface - as_column(at(total, ext + 1), tile_lon)
    east = wet * w_east * (east_speed - COURANT * (rows_cat([pressure[1:], p_east]) - pressure))
    east_west = w_west * wet[:1] * (u_west - COURANT * (pressure[:1] - p_west))
    east_flux = 0.5 * (depth + d_east) * east
    flux_west = 0.5 * (d_west + depth[:1]) * east_west
    north = wet * w_north * (north_speed - COURANT * (lanes_cat([pressure[:, 1:], p_north]) - pressure))
    north_south = s_wet * wet[:, :1] * (s_speed - COURANT * (pressure[:, :1] - p_south))
    north_flux = 0.5 * (depth + d_north) * north
    flux_south = jnp.where(y > 0, 0.5 * (s_depth + depth[:, :1]) * north_south, 0.0)
    east_out[...] = east
    north_out[...] = north
    next_out[...] = wet * (
        surface
        - COURANT
        * (
            east_flux
            - rows_cat([flux_west, east_flux[:-1]])
            + north_flux
            - lanes_cat([flux_south, north_flux[:, :-1]])
        )
    )
    for c in out1 + out2 + out3 + out4:
        c.wait_send()


def on_device(height, east_speed, north_speed, water_depth, ocean_mask, fold_partner, love_factor):
    tile_lon, tile_lat = height.shape
    degrees = love_factor.shape[0]
    gx = lax.axis_size("gx")
    gy = lax.axis_size("gy")
    lon_count = tile_lon * gx
    lat_count = tile_lat * gy
    half = lat_count // 2
    per = -(-degrees // (gx * gy))
    sp = -(-per // 16) * 16
    padded = -(-degrees // CHUNK) * CHUNK
    dims = (gx, gy, per, sp, padded)
    rows = 2 * sp
    ext = tile_lon + 8

    theta = np.pi * (np.arange(half) + 0.5) / lat_count
    quadrature = np.pi / lat_count * (2.0 * np.pi / lon_count) * np.sin(theta)
    lat_table = np.zeros((8, half), np.float32)
    lat_table[0], lat_table[1], lat_table[2] = np.cos(theta), np.log(np.sin(theta)), quadrature
    slots = per * gx * gy
    k = np.arange(1, slots, dtype=np.float64)
    logs = np.concatenate([[0.0], np.cumsum(0.5 * np.log((2.0 * k + 1.0) / (2.0 * k)))])
    ell = np.arange(padded, dtype=np.float64)
    root = np.sqrt(np.maximum(4.0 * ell * ell - 1.0, 1.0))
    ratio = root / np.sqrt(np.maximum(4.0 * (ell - 1.0) ** 2 - 1.0, 1.0))

    hbm = pl.BlockSpec(memory_space=pl.ANY)
    vmem = pl.BlockSpec(memory_space=pltpu.VMEM)
    smem = pl.BlockSpec(memory_space=pltpu.SMEM)
    tile = lambda *lead: pltpu.VMEM(lead + (tile_lat,), F32)
    dma = lambda n: pltpu.SemaphoreType.DMA((n,))
    return pl.pallas_call(
        functools.partial(step_kernel, dims),
        out_shape=[jax.ShapeDtypeStruct(height.shape, F32)] * 4,
        in_specs=[hbm] * 5 + [vmem] + [smem] * 5,
        out_specs=[vmem] * 4,
        scratch_shapes=[
            tile(tile_lon), tile(tile_lon), tile(tile_lon), tile(tile_lon),
            pltpu.VMEM((tile_lon, tile_lat), jnp.int32),
            pltpu.VMEM((padded * sp, half), BF16),
            pltpu.VMEM((padded * sp, half), BF16),
            tile(ext), tile(gx, ext),
            tile(gy, rows + 8), tile(gy, rows + 8),
            tile(gy, rows + 8), tile(gy, rows + 8),
            tile(gx, ext + 8), tile(gx, ext + 8),
            pltpu.VMEM((gx, ext, 2 * tile_lat), F32),
            dma(5), dma(gx), dma(gx), dma(gy), dma(gy), dma(gy), dma(gy), dma(gx), dma(gx),
        ],
        compiler_params=pltpu.CompilerParams(
            collective_id=0, has_side_effects=True, vmem_limit_bytes=48 * 2**20
        ),
    )(
        height, east_speed, north_speed, water_depth, ocean_mask, jnp.asarray(lat_table),
        fold_partner, love_factor,
        *(jnp.asarray(a.astype(np.float32)) for a in (logs, root, ratio)),
    )


def solution(mesh):
    spec = P("gx", "gy")
    return jax.shard_map(
        on_device, mesh=mesh, in_specs=(spec,) * 5 + (P(), P()), out_specs=(spec,) * 4, check_vma=False
    )
```

time: 73.5 us -> 45.3 us (0.62)
  Pallas kernels: 14.3 us -> 33.9 us
  starting transfers between devices: 13.4 us -> 0 us
  waiting for transfers between devices: 12.5 us -> 0 us
  blocking collectives: 10.8 us -> 0 us
  local copies, waits for them, and re-layouts: 13.9 us -> 10.2 us
  matrix products: 2.55 us -> 0 us
  between operations: 3.04 us -> 0.66 us
  other arithmetic: 2.22 us -> 0 us
    pallas_call x1, Pallas kernels: 14.3 us -> 33.9 us  [on_device(): pl.pallas_call(functools.partial(step_kernel, dims), out_shape=[jax.Shape...]
    all_to_all x3 -> x0, starting transfers between devices: 13.4 us -> none  [the longest x1 5.09 us: on_device(): lax.all_to_all(jnp.concatenate([grid_rows, rims], axis=1), 'gy', split_ax...]
    all_to_all x3 -> x0, waiting for transfers between devices: 12.5 us -> none  [the longest x1 6.72 us: on_device(): lax.all_to_all(jnp.concatenate([made[:, :, :tile_lat], rim], axis=1), 'gx...]
    all_gather x1 -> x0, blocking collectives: 10.8 us -> none  [on_device(): gathered = lax.all_gather(pack, 'gx', axis=0)]
    dot_general x2 -> x0, matrix products: 2.55 us -> none  [the longest x1 1.32 us: on_device(): jnp.dot(ahead, gathered[:, :tile_lon].reshape(lon_count, tile_lat), preci...]
    unnamed x34 -> x26, local copies, waits for them, and re-layouts: 8.16 us -> 10.2 us
    concatenate x6 -> x0, other arithmetic: 1.49 us -> none  [the longest x1 0.64 us: on_device(): jnp.concatenate([grid_rows, rims], axis=1)]
    dynamic_slice x5 -> x0, local copies, waits for them, and re-layouts: 1.45 us -> none  [the longest x1 0.76 us: on_device(): lax.dynamic_slice(jnp.asarray(logs.astype(np.float32)), (first,), (sp,))]
  transfers between devices with their start and end apart: 3 -> 0, of which waited for: 2 -> 0; matrix products, arithmetic and copies ran while one was open for 4% -> 0% of each run, Pallas kernels for 0% -> 0%
where the time goes in v2:
time: 45.3 us; the launch traced here: 44.8 us
  Pallas kernels  33.9 us (75%)
  local copies, waits for them, and re-layouts  10.2 us (23%)
  between operations  0.66 us (1%)
    pallas_call x1, Pallas kernels, on_device(): pl.pallas_call(functools.partial(step_kernel, dims), out_shape=[jax.Shape...  33.9 us
    unnamed x26, local copies, waits for them, and re-layouts  10.2 us

profile of v2, /device:TPU:0, one launch (start us, length us, event | category | flops | bytes accessed | tf_op | source)
XLA Modules:
  0.0 44.8 jit_solution(11296018763543703302)
XLA Ops:
  0.6 0.0 copy-start.7
  0.6 0.7 %copy-done.7 = f32[368]{0:T(512)S(1)} copy-done((f32[368]{0:T(512)S(1)}, f32[368]{0:T(512)}, u32[]{:S(2)}) %copy-start.7) | copy-done | bytes 1496
  1.3 0.0 copy-start
  1.3 0.7 %copy-done = f32[48,128]{1,0:T(8,128)S(1)} copy-done((f32[48,128]{1,0:T(8,128)S(1)}, f32[48,128]{1,0:T(8,128)}, u32[]{:S(2)}) %copy-start) | copy-done | bytes 24600
  2.1 0.0 copy-start.1
  2.1 0.7 %copy-done.1 = f32[48,128]{1,0:T(8,128)S(1)} copy-done((f32[48,128]{1,0:T(8,128)S(1)}, f32[48,128]{1,0:T(8,128)}, u32[]{:S(2)}) %copy-start.1) | copy-done | bytes 24600
  2.8 0.0 copy-start.2
  2.8 0.7 %copy-done.2 = f32[48,128]{1,0:T(8,128)S(1)} copy-done((f32[48,128]{1,0:T(8,128)S(1)}, f32[48,128]{1,0:T(8,128)}, u32[]{:S(2)}) %copy-start.2) | copy-done | bytes 24600
  3.5 0.0 copy-start.3
  3.5 0.7 %copy-done.3 = f32[48,128]{1,0:T(8,128)S(1)} copy-done((f32[48,128]{1,0:T(8,128)S(1)}, f32[48,128]{1,0:T(8,128)}, u32[]{:S(2)}) %copy-start.3) | copy-done | bytes 24600
  4.3 0.0 copy-start.4
  4.3 0.7 %copy-done.4 = s32[48,128]{1,0:T(8,128)S(1)} copy-done((s32[48,128]{1,0:T(8,128)S(1)}, s32[48,128]{1,0:T(8,128)}, u32[]{:S(2)}) %copy-start.4) | copy-done | bytes 24600
  5.0 0.0 copy-start.5
  5.0 0.7 %copy-done.5 = f32[8,256]{1,0:T(8,128)S(1)} copy-done((f32[8,256]{1,0:T(8,128)S(1)}, f32[8,256]{1,0:T(8,128)}, u32[]{:S(2)}) %copy-start.5) | copy-done | bytes 8216
  5.7 0.0 copy-start.6
  5.7 0.7 %copy-done.6 = f32[360]{0:T(512)S(1)} copy-done((f32[360]{0:T(512)S(1)}, f32[360]{0:T(512)}, u32[]{:S(2)}) %copy-start.6) | copy-done | bytes 1464
  6.4 0.7 %copy-done.8 = f32[368]{0:T(512)S(1)} copy-done((f32[368]{0:T(512)S(1)}, f32[368]{0:T(512)}, u32[]{:S(2)}) %copy-start.8) | copy-done | bytes 1496
  7.1 0.7 %copy-done.9 = f32[384]{0:T(512)S(1)} copy-done((f32[384]{0:T(512)S(1)}, f32[384]{0:T(512)}, u32[]{:S(2)}) %copy-start.9) | copy-done | bytes 1560
  7.8 0.7 %copy-done.10 = s32[8]{0:T(128)S(1)} copy-done((s32[8]{0:T(128)S(1)}, s32[8]{0:T(128)}, u32[]{:S(2)}) %copy-start.10) | copy-done | bytes 56
  8.4 33.9 %shard_map.138 = (f32[48,128]{1,0:T(8,128)S(1)}, f32[48,128]{1,0:T(8,128)S(1)}, f32[48,128]{1,0:T(8,128)S(1)}, f32[48,128]{1,0:T(8,128)S(1)}) custom-call(f32[48,128]{1,0:T(8,128)S(1)} %copy-done, f32[48,128]{1,0:T(8,128)S(1)} %copy-done.1, f32[48,128]{1,0:T(8,128)S(1)} %copy-done.2, f32[48,128]{1,0:T(8,128)S(1)} %copy-done.3, s32[48,128]{1,0:T(8,128)S(1)} %copy-done.4, ...), custom_call_target="tpu_custom_call" | custom-call | tf_op jit(solution)/shard_map/pallas_call | solution.py:415
  42.3 0.6 %copy.19 = f32[48,128]{1,0:T(8,128)} copy(f32[48,128]{1,0:T(8,128)S(1)} %get-tuple-element.8) | data formatting | bytes 49152
  42.9 0.6 %copy.20 = f32[48,128]{1,0:T(8,128)} copy(f32[48,128]{1,0:T(8,128)S(1)} %get-tuple-element.9) | data formatting | bytes 49152
  43.5 0.6 %copy.21 = f32[48,128]{1,0:T(8,128)} copy(f32[48,128]{1,0:T(8,128)S(1)} %get-tuple-element.10) | data formatting | bytes 49152
  44.1 0.6 %copy.22 = f32[48,128]{1,0:T(8,128)} copy(f32[48,128]{1,0:T(8,128)S(1)} %get-tuple-element.11) | data formatting | bytes 49152
  (3 shorter events, 0.0 us)
Async XLA Ops:
  0.6 0.7 %copy-start.7 = (f32[368]{0:T(512)S(1)}, f32[368]{0:T(512)}, u32[]{:S(2)}) copy-start(f32[368]{0:T(512)} %constant.11.clone.ratio_ref) | copy-start | bytes 4420
  1.3 0.7 %copy-start = (f32[48,128]{1,0:T(8,128)S(1)}, f32[48,128]{1,0:T(8,128)}, u32[]{:S(2)}) copy-start(f32[48,128]{1,0:T(8,128)} %height_hbm.1) | copy-start | bytes 73732
  2.1 0.7 %copy-start.1 = (f32[48,128]{1,0:T(8,128)S(1)}, f32[48,128]{1,0:T(8,128)}, u32[]{:S(2)}) copy-start(f32[48,128]{1,0:T(8,128)} %east_hbm.1) | copy-start | bytes 73732
  2.8 0.7 %copy-start.2 = (f32[48,128]{1,0:T(8,128)S(1)}, f32[48,128]{1,0:T(8,128)}, u32[]{:S(2)}) copy-start(f32[48,128]{1,0:T(8,128)} %north_hbm.1) | copy-start | bytes 73732
  3.5 0.7 %copy-start.3 = (f32[48,128]{1,0:T(8,128)S(1)}, f32[48,128]{1,0:T(8,128)}, u32[]{:S(2)}) copy-start(f32[48,128]{1,0:T(8,128)} %depth_hbm.1) | copy-start | bytes 73732
  4.3 0.7 %copy-start.4 = (s32[48,128]{1,0:T(8,128)S(1)}, s32[48,128]{1,0:T(8,128)}, u32[]{:S(2)}) copy-start(s32[48,128]{1,0:T(8,128)} %mask_hbm.1) | copy-start | bytes 73732
  5.0 0.7 %copy-start.5 = (f32[8,256]{1,0:T(8,128)S(1)}, f32[8,256]{1,0:T(8,128)}, u32[]{:S(2)}) copy-start(f32[8,256]{1,0:T(8,128)} %constant.8.clone.lat_ref) | copy-start | bytes 24580
  5.7 0.7 %copy-start.6 = (f32[360]{0:T(512)S(1)}, f32[360]{0:T(512)}, u32[]{:S(2)}) copy-start(f32[360]{0:T(512)} %love_ref.1) | copy-start | bytes 4324
  6.4 0.7 %copy-start.8 = (f32[368]{0:T(512)S(1)}, f32[368]{0:T(512)}, u32[]{:S(2)}) copy-start(f32[368]{0:T(512)} %constant.10.clone.root_ref) | copy-start | bytes 4420
  7.1 0.7 %copy-start.9 = (f32[384]{0:T(512)S(1)}, f32[384]{0:T(512)}, u32[]{:S(2)}) copy-start(f32[384]{0:T(512)} %constant.9.clone.logs_ref) | copy-start | bytes 4612
  7.8 0.7 %copy-start.10 = (s32[8]{0:T(128)S(1)}, s32[8]{0:T(128)}, u32[]{:S(2)}) copy-start(s32[8]{0:T(128)} %fold_ref.1) | copy-start | bytes 100
